TPU v7x, 512 devices: a whole 4x8x8 slice. The times are simulated.
512 devices in a mesh: inst: 64 (over z, x, core), tp: 8 (over y).
Axes of the slice: x: 4, y: 8, z: 8, core: 2. Of those that a mesh axis runs over, the one named last changes fastest.
Arguments:
- queries: bfloat16 [64, 4096], P('inst', 'tp'), may hold values from -360 to 360
- slot_request: int32 [64], P('inst'), may hold values from -1 to 31, as said below
- key_cache_pages: bfloat16 [2048, 128, 1024], P('inst', None, 'tp'), may hold values from -6 to 6
- value_cache_pages: bfloat16 [2048, 128, 1024], P('inst', None, 'tp'), may hold values from -6 to 6
- page_owner: int32 [2048], P('inst'), may hold values from -1 to 31, as said below
- page_fill: int32 [2048], P('inst'), may hold values from 1 to 128
- out_weight: bfloat16 [4096, 4096], P('tp', 'inst'), may hold values from -0.09375 to 0.09375
Outputs:
- projected: bfloat16 [64, 4096], P('inst', 'tp')
Inputs may be any that keep to these rules, and one draw needn't show every extreme that they name: `slot_request`: each request id appears in exactly one slot; every other slot holds -1. `page_owner`: each entry is -1 (a free page) or a request id; every request owns at least one page.
All inputs are finite; a program needn't handle non-finite values.
Results may differ from a plain program's by a relative error of at most 0.005.
Values may be sent and summed in bfloat16 or wider, within the bound.
No kernel may reach another device: no remote copies, remote signals or barrier semaphores. Data moves between devices by JAX's collectives and lax.ppermute only.
A program may use at most 64 MiB of HBM per device.

v0:
```python
import jax
import jax.numpy as jnp
from jax import lax
from jax.sharding import PartitionSpec as P

HEAD_SIZE = 128
NEG_FILL = -1e30


def sent_to_all(x, axis):
    length = lax.axis_size(axis)
    return lax.all_to_all(jnp.broadcast_to(x[None], (length, *x.shape)), axis, 0, 0, tiled=True)


def in_order(parts, dim):
    parts = jnp.moveaxis(parts, 0, dim)
    dims = parts.shape
    return parts.reshape(*dims[:dim], dims[dim] * dims[dim + 1], *dims[dim + 2 :])


def collect(x, axis, dim):
    parts = sent_to_all(x, axis)
    return in_order(parts, dim)


def taken_together(x, axis):
    everything = sent_to_all(x, axis)
    return jnp.max(everything, axis=0)


def split_up(x, dim, length):
    before, after = (x.shape[:dim], x.shape[dim + 1 :])
    return jnp.moveaxis(x.reshape(*before, length, -1, *after), dim, 0)


def summed_on_arrival(x, axis, dim):
    parts = split_up(x, dim, lax.axis_size(axis))
    arrived = lax.all_to_all(parts, axis, split_axis=0, concat_axis=0, tiled=True)
    return arrived.sum(axis=0)


def in_one_piece(arrays, axis, dim, along):
    both = jnp.concatenate(arrays, axis=along)
    result, at, finished = (summed_on_arrival(both, axis, dim), 0, [])
    for a in arrays:
        finished.append(lax.slice_in_dim(result, at, at + a.shape[along], axis=along))
        at += a.shape[along]
    return tuple(finished)


def on_device(
    queries, slot_request, key_cache_pages, value_cache_pages, page_owner, page_fill, out_weight
):
    whole_q, whole_req = (collect(queries, "inst", 0), collect(slot_request, "inst", 0))
    n_pages, page_len, kv_width = key_cache_pages.shape
    kv_local = kv_width // HEAD_SIZE
    q_local = whole_q.shape[1] // HEAD_SIZE
    query_group = q_local // kv_local
    n_slots = whole_q.shape[0]
    n_inst = lax.axis_size("inst")
    slots_dev = n_slots // n_inst
    owner_match = (page_owner[:, None] == whole_req[None, :]) & (whole_req[None, :] >= 0)
    selected_pages = jnp.dot(
        owner_match.astype(jnp.bfloat16), whole_q, preferred_element_type=jnp.float32
    ).astype(jnp.bfloat16)
    query_portion = selected_pages.reshape(n_pages, kv_local, query_group, HEAD_SIZE)
    key_portion = key_cache_pages.reshape(n_pages, page_len, kv_local, HEAD_SIZE)
    value_portion = value_cache_pages.reshape(n_pages, page_len, kv_local, HEAD_SIZE)
    scores = jnp.einsum(
        "pkgd,ptkd->pkgt", query_portion, key_portion, preferred_element_type=jnp.float32
    ) * HEAD_SIZE ** (-0.5)
    positions = jnp.arange(page_len, dtype=jnp.int32)
    is_valid = positions[None, None, None, :] < page_fill[:, None, None, None]
    scores = jnp.where(is_valid, scores, NEG_FILL)
    page_peak = jnp.max(scores, axis=-1)
    expo_vals = jnp.exp(scores - page_peak[..., None])
    page_total = jnp.sum(expo_vals, axis=-1).reshape(n_pages, q_local)
    prob_bf = expo_vals.astype(jnp.bfloat16)
    page_out = jnp.einsum(
        "pkgt,ptkd->pkgd", prob_bf, value_portion, preferred_element_type=jnp.float32
    )
    page_out = page_out.reshape(n_pages, q_local, HEAD_SIZE)
    page_peak = page_peak.reshape(n_pages, q_local)
    chosen = owner_match[:, :, None]
    slot_peak = jnp.max(jnp.where(chosen, page_peak[:, None, :], NEG_FILL), axis=0)
    weight = jnp.exp(jnp.where(chosen, page_peak[:, None, :] - slot_peak[None], NEG_FILL))
    slot_total = jnp.sum(weight * page_total[:, None, :], axis=0)
    slot_mix = jnp.einsum("prh,phd->rhd", weight, page_out, precision=lax.Precision.HIGHEST)
    global_peak = taken_together(slot_peak, "inst")
    factor = jnp.exp(slot_peak - global_peak)
    share_mix, share_total = in_one_piece(
        ((slot_mix * factor[..., None]).reshape(n_slots, q_local * HEAD_SIZE), slot_total * factor),
        "inst",
        0,
        1,
    )
    divisor = jnp.where(share_total > 0.0, share_total, 1.0)
    attention = (
        (share_mix.reshape(slots_dev, q_local, HEAD_SIZE) / divisor[..., None])
        .reshape(slots_dev, q_local * HEAD_SIZE)
        .astype(jnp.bfloat16)
    )
    every_row = collect(attention, "inst", 0)
    column_part = jnp.dot(every_row, out_weight, preferred_element_type=jnp.float32)
    partial_value = lax.all_to_all(column_part, "inst", split_axis=0, concat_axis=1, tiled=True)
    return summed_on_arrival(partial_value, "tp", 1).astype(jnp.bfloat16)


def solution(mesh):
    return jax.shard_map(
        on_device,
        mesh=mesh,
        in_specs=(
            P("inst", "tp"),
            P("inst"),
            P("inst", None, "tp"),
            P("inst", None, "tp"),
            P("inst"),
            P("inst"),
            P("tp", "inst"),
        ),
        out_specs=P("inst", "tp"),
        check_vma=False,
    )
```

profile of v0, /device:TPU:1, one launch (start us, length us, event | category | flops | bytes accessed | tf_op | source)
XLA Modules:
  0.0 119.8 jit_solution(11090895609242776855)
XLA Ops:
  0.7 0.6 broadcast_in_dim.82
  1.4 15.0 %all-to-all-start = ((s32[64,1,1]{2,1,0:T(1,128)}), s32[64,1,1]{2,1,0:T(1,128)S(1)}, u32[]{:S(2)}, u32[]{:S(2)}) async-start(s32[64,1,1]{2,1,0:T(1,128)} %broadcast_in_dim.82), calls=%async_computation | async-start | bytes 65536 | tf_op jit(solution)/shard_map/all_to_all | solution.py:12
  16.4 0.6 copy-done.4
  17.1 0.5 broadcast.77
  17.6 1.0 reduce.14
  18.6 0.6 reshape.189
  19.3 6.4 %all-to-all-done = s32[64,1,1]{2,1,0:T(1,128)S(1)} async-done(((s32[64,1,1]{2,1,0:T(1,128)}), s32[64,1,1]{2,1,0:T(1,128)S(1)}, u32[]{:S(2)}, u32[]{:S(2)}) %all-to-all-start) | async-done | bytes 288 | tf_op jit(solution)/shard_map/all_to_all | solution.py:12
  25.7 4.8 %all-to-all-start.1 = ((bf16[64,2,256]{2,1,0:T(2,128)(2,1)}), bf16[64,2,256]{2,1,0:T(2,128)(2,1)S(1)}, u32[]{:S(2)}, u32[]{:S(2)}) async-start(bf16[64,2,256]{2,1,0:T(2,128)(2,1)} %reshape.189), calls=%async_computation.1 | async-start | bytes 131072 | tf_op jit(solution)/shard_map/all_to_all | solution.py:12
  30.6 1.2 %reduce.6 = s32[64]{0:T(128)S(1)} reduce(s32[64,1,1]{2,1,0:T(1,128)S(1)} %all-to-all-done, s32[]{:T(128)} %constant.6.clone.1), dimensions={1,2}, to_apply=%all_to_all.29.reduce_sub_computation | reduce | bytes 516 | tf_op jit(solution)/shard_map/all_to_all | solution.py:12
  31.9 8.8 %all-to-all-done.1 = bf16[64,2,256]{2,1,0:T(2,128)(2,1)S(1)} async-done(((bf16[64,2,256]{2,1,0:T(2,128)(2,1)}), bf16[64,2,256]{2,1,0:T(2,128)(2,1)S(1)}, u32[]{:S(2)}, u32[]{:S(2)}) %all-to-all-start.1) | async-done | bytes 65568 | tf_op jit(solution)/shard_map/all_to_all | solution.py:12
  40.7 0.2 convolution_convert_fusion
  41.0 0.7 fusion.21
  41.9 0.8 reshape.191
  42.7 4.4 %all-to-all-start.2 = ((f32[64,1,256]{2,1,0:T(1,128)}), f32[64,1,256]{2,1,0:T(1,128)S(1)}, u32[]{:S(2)}, u32[]{:S(2)}) async-start(f32[64,1,256]{2,1,0:T(1,128)} %reshape.191), calls=%async_computation.2 | async-start | bytes 131072 | tf_op jit(solution)/shard_map/all_to_all | solution.py:12
  47.1 0.4 fusion.11
  47.6 0.2 fusion.9
  48.0 9.3 %all-to-all-done.2 = f32[64,1,256]{2,1,0:T(1,128)S(1)} async-done(((f32[64,1,256]{2,1,0:T(1,128)}), f32[64,1,256]{2,1,0:T(1,128)S(1)}, u32[]{:S(2)}, u32[]{:S(2)}) %all-to-all-start.2) | async-done | bytes 65568 | tf_op jit(solution)/shard_map/all_to_all | solution.py:12
  57.2 0.6 broadcast.78
  57.8 0.8 reduce.15
  58.9 0.5 fusion.1
  59.5 0.2 copy.28
  59.7 15.4 %all_to_all.44 = f32[64,1,516]{2,1,0:T(1,128)S(1)} all-to-all(f32[64,1,516]{2,1,0:T(1,128)S(1)} %copy.28), channel_id=1, replica_groups=mesh['inst'=64,'tp'=8] {'inst'}, dimensions={0} | all-to-all | bytes 264192 | tf_op jit(solution)/shard_map/all_to_all | solution.py:38
  75.1 0.1 reduce_sum.40
  75.4 1.0 reduce.16
  76.5 14.0 %all_to_all.45 = bf16[64,2,256]{2,1,0:T(2,128)(2,1)S(1)} all-to-all(bf16[64,2,256]{2,1,0:T(2,128)(2,1)S(1)} %reshape.193), channel_id=1, replica_groups=mesh['inst'=64,'tp'=8] {'inst'}, dimensions={0} | all-to-all | bytes 131072 | tf_op jit(solution)/shard_map/all_to_all | solution.py:12
  90.5 0.8 copy-done.2
  91.3 0.1 fusion.3
  91.4 13.1 %all_to_all.46 = f32[64,1,64]{2,1,0:T(1,128)S(1)} all-to-all(f32[64,1,64]{2,1,0:T(1,128)S(1)} %bitcast.36), channel_id=1, replica_groups=mesh['inst'=64,'tp'=8] {'inst'}, dimensions={0} | all-to-all | bytes 32768 | tf_op jit(solution)/shard_map/all_to_all | solution.py:105
  104.6 0.5 broadcast.76
  105.1 0.7 reduce.13
  105.9 13.2 %all_to_all.47 = f32[8,1,512]{2,1,0:T(1,128)S(1)} all-to-all(f32[8,1,512]{2,1,0:T(1,128)S(1)} %transpose_reshape.4), channel_id=1, replica_groups=mesh['inst'=64,'tp'=8] {'tp'}, dimensions={0} | all-to-all | bytes 32768 | tf_op jit(solution)/shard_map/all_to_all | solution.py:38
  119.2 0.6 convert_element_type.31
  (37 shorter events, 1.5 us)
Async XLA Ops:
  0.0 41.0 %copy-start = (bf16[32,128,128]{2,1,0:T(8,128)(2,1)S(1)}, bf16[32,128,128]{2,1,0:T(8,128)(2,1)}, u32[]{:S(2)}) copy-start(bf16[32,128,128]{2,1,0:T(8,128)(2,1)} %param.9) | copy-start | bytes 3145732
  1.4 15.0 %copy-start.5 = (s32[32]{0:T(128)S(1)}, s32[32]{0:T(128)}, u32[]{:S(2)}) copy-start(s32[32]{0:T(128)} %param.12) | copy-start | bytes 388
  1.4 24.4 %all-to-all-start = ((s32[64,1,1]{2,1,0:T(1,128)}), s32[64,1,1]{2,1,0:T(1,128)S(1)}, u32[]{:S(2)}, u32[]{:S(2)}) async-start(s32[64,1,1]{2,1,0:T(1,128)} %broadcast_in_dim.82), calls=%async_computation | async-start | bytes 65536 | tf_op jit(solution)/shard_map/all_to_all | solution.py:12
  16.3 0.7 copy-start.4
  25.7 6.1 %copy-start.3 = (s32[32]{0:T(128)S(1)}, s32[32]{0:T(128)}, u32[]{:S(2)}) copy-start(s32[32]{0:T(128)} %param.11) | copy-start | bytes 388
  25.7 15.0 %all-to-all-start.1 = ((bf16[64,2,256]{2,1,0:T(2,128)(2,1)}), bf16[64,2,256]{2,1,0:T(2,128)(2,1)S(1)}, u32[]{:S(2)}, u32[]{:S(2)}) async-start(bf16[64,2,256]{2,1,0:T(2,128)(2,1)} %reshape.189), calls=%async_computation.1 | async-start | bytes 131072 | tf_op jit(solution)/shard_map/all_to_all | solution.py:12
  30.6 16.5 %copy-start.1 = (bf16[32,128,128]{2,1,0:T(8,128)(2,1)S(1)}, bf16[32,128,128]{2,1,0:T(8,128)(2,1)}, u32[]{:S(2)}) copy-start(bf16[32,128,128]{2,1,0:T(8,128)(2,1)} %param.10) | copy-start | bytes 3145732
  42.7 14.6 %all-to-all-start.2 = ((f32[64,1,256]{2,1,0:T(1,128)}), f32[64,1,256]{2,1,0:T(1,128)S(1)}, u32[]{:S(2)}, u32[]{:S(2)}) async-start(f32[64,1,256]{2,1,0:T(1,128)} %reshape.191), calls=%async_computation.2 | async-start | bytes 131072 | tf_op jit(solution)/shard_map/all_to_all | solution.py:12
  90.5 0.8 copy-start.2
where the time goes:
time: 120 us
  blocking collectives  55.8 us (46%)
  waiting for transfers between devices  24.5 us (20%)
  starting transfers between devices  24.2 us (20%)
  local copies, waits for them, and re-layouts  6.63 us (6%)
  other arithmetic  5.72 us (5%)
  matrix products  1.98 us (2%)
    all_to_all x2, blocking collectives, summed_on_arrival(): lax.all_to_all(parts, axis, split_axis=0, concat_axis=0, tiled=True)  28.6 us
    all_to_all x3, waiting for transfers between devices, sent_to_all(): lax.all_to_all(jnp.broadcast_to(x[None], (length, *x.shape)), axis, 0, 0,...  24.5 us
    all_to_all x3, starting transfers between devices, sent_to_all(): lax.all_to_all(jnp.broadcast_to(x[None], (length, *x.shape)), axis, 0, 0,...  24.2 us
    all_to_all x1, blocking collectives, sent_to_all(): lax.all_to_all(jnp.broadcast_to(x[None], (length, *x.shape)), axis, 0, 0,...  14 us
    all_to_all x1, blocking collectives, on_device(): lax.all_to_all(column_part, 'inst', split_axis=0, concat_axis=1, tiled=True)  13.1 us
    unnamed x19, local copies, waits for them, and re-layouts  3.06 us
  transfers between devices with their start and end apart: 3, of which 3 were waited for; matrix products, arithmetic and copies ran while one was open for 4% of the time, Pallas kernels for 0%

commit v1 on v0

--- a/solution.py
+++ b/solution.py
@@ -102,7 +102,12 @@
     )
     every_row = collect(attention, "inst", 0)
     column_part = jnp.dot(every_row, out_weight, preferred_element_type=jnp.float32)
-    partial_value = lax.all_to_all(column_part, "inst", split_axis=0, concat_axis=1, tiled=True)
+    partial_value = jnp.concatenate(
+        lax.all_to_all(
+            jnp.stack(jnp.split(column_part, lax.axis_size("inst"), axis=0)), "inst", 0, 0
+        ),
+        axis=1,
+    )
     return summed_on_arrival(partial_value, "tp", 1).astype(jnp.bfloat16)
 
 

time: 120 us -> 121 us (level)
    unnamed x19 -> x82, local copies, waits for them, and re-layouts: 3.06 us -> 3.7 us
where the time goes in v1:
time: 121 us
  blocking collectives  55.8 us (46%)
  waiting for transfers between devices  24.5 us (20%)
  starting transfers between devices  24.2 us (20%)
  local copies, waits for them, and re-layouts  7.29 us (6%)
  other arithmetic  5.72 us (5%)
  matrix products  1.98 us (2%)
    all_to_all x2, blocking collectives, summed_on_arrival(): lax.all_to_all(parts, axis, split_axis=0, concat_axis=0, tiled=True)  28.6 us
    all_to_all x3, waiting for transfers between devices, sent_to_all(): lax.all_to_all(jnp.broadcast_to(x[None], (length, *x.shape)), axis, 0, 0,...  24.5 us
    all_to_all x3, starting transfers between devices, sent_to_all(): lax.all_to_all(jnp.broadcast_to(x[None], (length, *x.shape)), axis, 0, 0,...  24.2 us
    all_to_all x1, blocking collectives, sent_to_all(): lax.all_to_all(jnp.broadcast_to(x[None], (length, *x.shape)), axis, 0, 0,...  14 us
    all_to_all x1, blocking collectives, on_device(): lax.all_to_all(jnp.stack(jnp.split(column_part, lax.axis_size('inst'), ax...  13.1 us
    unnamed x82, local copies, waits for them, and re-layouts  3.7 us
  transfers between devices with their start and end apart: 3, of which 3 were waited for; matrix products, arithmetic and copies ran while one was open for 4% of the time, Pallas kernels for 0%

profile of v1, /device:TPU:1, one launch (start us, length us, event | category | flops | bytes accessed | tf_op | source)
XLA Modules:
  0.0 120.6 jit_solution(10245821674199624380)
XLA Ops:
  0.7 0.6 broadcast_in_dim.82
  1.4 15.0 %all-to-all-start = ((s32[64,1,1]{2,1,0:T(1,128)}), s32[64,1,1]{2,1,0:T(1,128)S(1)}, u32[]{:S(2)}, u32[]{:S(2)}) async-start(s32[64,1,1]{2,1,0:T(1,128)} %broadcast_in_dim.82), calls=%async_computation | async-start | bytes 65536 | tf_op jit(solution)/shard_map/all_to_all | solution.py:12
  16.4 0.6 copy-done.4
  17.1 0.5 broadcast.77
  17.6 1.0 reduce.14
  18.6 0.6 reshape.182
  19.3 6.4 %all-to-all-done = s32[64,1,1]{2,1,0:T(1,128)S(1)} async-done(((s32[64,1,1]{2,1,0:T(1,128)}), s32[64,1,1]{2,1,0:T(1,128)S(1)}, u32[]{:S(2)}, u32[]{:S(2)}) %all-to-all-start) | async-done | bytes 288 | tf_op jit(solution)/shard_map/all_to_all | solution.py:12
  25.7 4.8 %all-to-all-start.1 = ((bf16[64,2,256]{2,1,0:T(2,128)(2,1)}), bf16[64,2,256]{2,1,0:T(2,128)(2,1)S(1)}, u32[]{:S(2)}, u32[]{:S(2)}) async-start(bf16[64,2,256]{2,1,0:T(2,128)(2,1)} %reshape.182), calls=%async_computation.1 | async-start | bytes 131072 | tf_op jit(solution)/shard_map/all_to_all | solution.py:12
  30.6 1.2 %reduce.6 = s32[64]{0:T(128)S(1)} reduce(s32[64,1,1]{2,1,0:T(1,128)S(1)} %all-to-all-done, s32[]{:T(128)} %constant.6.clone.1), dimensions={1,2}, to_apply=%all_to_all.22.reduce_sub_computation | reduce | bytes 516 | tf_op jit(solution)/shard_map/all_to_all | solution.py:12
  31.9 8.8 %all-to-all-done.1 = bf16[64,2,256]{2,1,0:T(2,128)(2,1)S(1)} async-done(((bf16[64,2,256]{2,1,0:T(2,128)(2,1)}), bf16[64,2,256]{2,1,0:T(2,128)(2,1)S(1)}, u32[]{:S(2)}, u32[]{:S(2)}) %all-to-all-start.1) | async-done | bytes 65568 | tf_op jit(solution)/shard_map/all_to_all | solution.py:12
  40.7 0.2 convolution_convert_fusion
  41.0 0.7 fusion.21
  41.9 0.8 reshape.184
  42.7 4.4 %all-to-all-start.2 = ((f32[64,1,256]{2,1,0:T(1,128)}), f32[64,1,256]{2,1,0:T(1,128)S(1)}, u32[]{:S(2)}, u32[]{:S(2)}) async-start(f32[64,1,256]{2,1,0:T(1,128)} %reshape.184), calls=%async_computation.2 | async-start | bytes 131072 | tf_op jit(solution)/shard_map/all_to_all | solution.py:12
  47.1 0.4 fusion.11
  47.6 0.2 fusion.9
  48.0 9.3 %all-to-all-done.2 = f32[64,1,256]{2,1,0:T(1,128)S(1)} async-done(((f32[64,1,256]{2,1,0:T(1,128)}), f32[64,1,256]{2,1,0:T(1,128)S(1)}, u32[]{:S(2)}, u32[]{:S(2)}) %all-to-all-start.2) | async-done | bytes 65568 | tf_op jit(solution)/shard_map/all_to_all | solution.py:12
  57.2 0.6 broadcast.78
  57.8 0.8 reduce.15
  58.9 0.5 fusion.1
  59.5 0.2 copy.27
  59.7 15.4 %all_to_all.36 = f32[64,1,516]{2,1,0:T(1,128)S(1)} all-to-all(f32[64,1,516]{2,1,0:T(1,128)S(1)} %copy.27), channel_id=1, replica_groups=mesh['inst'=64,'tp'=8] {'inst'}, dimensions={0} | all-to-all | bytes 264192 | tf_op jit(solution)/shard_map/all_to_all | solution.py:38
  75.1 0.1 reduce_sum.40
  75.4 1.0 reduce.16
  76.5 14.0 %all_to_all.37 = bf16[64,2,256]{2,1,0:T(2,128)(2,1)S(1)} all-to-all(bf16[64,2,256]{2,1,0:T(2,128)(2,1)S(1)} %reshape.186), channel_id=1, replica_groups=mesh['inst'=64,'tp'=8] {'inst'}, dimensions={0} | all-to-all | bytes 131072 | tf_op jit(solution)/shard_map/all_to_all | solution.py:12
  90.5 0.8 copy-done.2
  91.3 0.1 fusion.3
  92.3 13.1 %all_to_all.38 = f32[64,1,64]{2,1,0:T(1,128)S(1)} all-to-all(f32[64,1,64]{2,1,0:T(1,128)S(1)} %constant_dynamic-update-slice_fusion), channel_id=1, replica_groups=mesh['inst'=64,'tp'=8] {'inst'}, dimensions={0} | all-to-all | bytes 32768 | tf_op jit(solution)/shard_map/all_to_all | solution.py:106
  105.4 0.5 broadcast.76
  105.9 0.7 reduce.13
  106.8 13.2 %all_to_all.39 = f32[8,1,512]{2,1,0:T(1,128)S(1)} all-to-all(f32[8,1,512]{2,1,0:T(1,128)S(1)} %transpose_reshape_reshape.4), channel_id=1, replica_groups=mesh['inst'=64,'tp'=8] {'tp'}, dimensions={0} | all-to-all | bytes 32768 | tf_op jit(solution)/shard_map/all_to_all | solution.py:38
  120.0 0.6 convert_element_type.31
  (101 shorter events, 2.1 us)
Async XLA Ops:
  0.0 41.0 %copy-start = (bf16[32,128,128]{2,1,0:T(8,128)(2,1)S(1)}, bf16[32,128,128]{2,1,0:T(8,128)(2,1)}, u32[]{:S(2)}) copy-start(bf16[32,128,128]{2,1,0:T(8,128)(2,1)} %param.9) | copy-start | bytes 3145732
  1.4 15.0 %copy-start.5 = (s32[32]{0:T(128)S(1)}, s32[32]{0:T(128)}, u32[]{:S(2)}) copy-start(s32[32]{0:T(128)} %param.12) | copy-start | bytes 388
  1.4 24.4 %all-to-all-start = ((s32[64,1,1]{2,1,0:T(1,128)}), s32[64,1,1]{2,1,0:T(1,128)S(1)}, u32[]{:S(2)}, u32[]{:S(2)}) async-start(s32[64,1,1]{2,1,0:T(1,128)} %broadcast_in_dim.82), calls=%async_computation | async-start | bytes 65536 | tf_op jit(solution)/shard_map/all_to_all | solution.py:12
  16.3 0.7 copy-start.4
  25.7 6.1 %copy-start.3 = (s32[32]{0:T(128)S(1)}, s32[32]{0:T(128)}, u32[]{:S(2)}) copy-start(s32[32]{0:T(128)} %param.11) | copy-start | bytes 388
  25.7 15.0 %all-to-all-start.1 = ((bf16[64,2,256]{2,1,0:T(2,128)(2,1)}), bf16[64,2,256]{2,1,0:T(2,128)(2,1)S(1)}, u32[]{:S(2)}, u32[]{:S(2)}) async-start(bf16[64,2,256]{2,1,0:T(2,128)(2,1)} %reshape.182), calls=%async_computation.1 | async-start | bytes 131072 | tf_op jit(solution)/shard_map/all_to_all | solution.py:12
  30.6 16.5 %copy-start.1 = (bf16[32,128,128]{2,1,0:T(8,128)(2,1)S(1)}, bf16[32,128,128]{2,1,0:T(8,128)(2,1)}, u32[]{:S(2)}) copy-start(bf16[32,128,128]{2,1,0:T(8,128)(2,1)} %param.10) | copy-start | bytes 3145732
  42.7 14.6 %all-to-all-start.2 = ((f32[64,1,256]{2,1,0:T(1,128)}), f32[64,1,256]{2,1,0:T(1,128)S(1)}, u32[]{:S(2)}, u32[]{:S(2)}) async-start(f32[64,1,256]{2,1,0:T(1,128)} %reshape.184), calls=%async_computation.2 | async-start | bytes 131072 | tf_op jit(solution)/shard_map/all_to_all | solution.py:12
  90.5 0.8 copy-start.2
